TPU v7x, 32 devices: a whole 2x2x4 slice. The times are simulated.
32 devices in a mesh: seq: 8 (over z, y), ch: 4 (over x, core).
Axes of the slice: x: 2, y: 2, z: 4, core: 2. Of those that a mesh axis runs over, the one named last changes fastest.
Arguments:
- inputs: bfloat16 [8192, 768], P(('seq', 'ch')), may hold values from -6 to 6
- gain_one: float32 [768], replicated, may hold values from 0.5 to 1.5
- shift_one: float32 [768], replicated, may hold values from -1.5 to 1.5
- conv_weight: bfloat16 [3, 768, 384], P(None, None, 'ch'), may hold values from -0.125 to 0.125
- gain_two: float32 [384], P('ch'), may hold values from 0.5 to 1.5
- shift_two: float32 [384], P('ch'), may hold values from -1.5 to 1.5
- mix_weight: bfloat16 [384, 768], P('ch'), may hold values from -0.3125 to 0.3125
- head_weight: bfloat16 [768, 6956], P('ch'), may hold values from -0.21875 to 0.21875
- head_bias: float32 [6956], replicated, may hold values from -2 to 2
- species: int32 [8], replicated, may hold values from 0 to 1, as said below
- counts: int32 [8192, 5313], P(('seq', 'ch')), may hold values from 0 to 3
Outputs:
- outputs: bfloat16 [8192, 768], P(('seq', 'ch'))
- input_grad: float32 [8192, 768], P(('seq', 'ch'))
- gain_one_grad: float32 [768], replicated
- shift_one_grad: float32 [768], replicated
- conv_weight_grad: float32 [3, 768, 384], P(None, None, 'ch')
- gain_two_grad: float32 [384], P('ch')
- shift_two_grad: float32 [384], P('ch')
- mix_weight_grad: float32 [384, 768], P('ch')
- head_weight_grad: float32 [768, 6956], P(('seq', 'ch'))
- head_bias_grad: float32 [6956], replicated
Inputs may be any that keep to these rules, and one draw needn't show every extreme that they name: Each window holds one species, given by species[w]; both species occur in every draw.
All inputs are finite; a program needn't handle non-finite values.
Results may differ from a plain program's by a relative error of at most 0.014.
Values may be sent and summed in bfloat16 or wider, within the bound.
A program may use at most 192 MiB of HBM per device.

v0:
```python
import jax
import jax.numpy as jnp
from jax import lax
from jax.sharding import PartitionSpec as P

HUMAN = 5313
MOUSE = 1643
DILATION_STEP = 11
TAPS = 3
WINDOW_BINS = 1024
SHIFT = 512
norm_eps = 1e-05
contract_rows = (((0,), (0,)), ((), ()))
contract_cols = (((1,), (1,)), ((), ()))


def with_halo(cells, sides, width):
    for axis, dim in sides:
        count = lax.axis_size(axis)
        head = lax.slice_in_dim(cells, 0, width, axis=dim)
        tail = lax.slice_in_dim(cells, cells.shape[dim] - width, cells.shape[dim], axis=dim)
        cells = jnp.concatenate(
            [
                lax.ppermute(tail, axis, [(i, (i + 1) % count) for i in range(count)]),
                cells,
                lax.ppermute(head, axis, [((i + 1) % count, i) for i in range(count)]),
            ],
            axis=dim,
        )
    return cells


def window_lookup(position, total_bins):
    return jnp.mod(position - SHIFT, total_bins) // WINDOW_BINS


def gelu_grad(value, upstream):
    _, pullback = jax.vjp(jax.nn.gelu, value)
    return pullback(upstream)[0]


def poisson_grad(logits, target):
    rate = jax.nn.softplus(logits)
    return (jax.nn.sigmoid(logits) * (1.0 - target / rate)).astype(jnp.bfloat16)


def on_device(
    inputs,
    gain_one,
    shift_one,
    conv_weight,
    gain_two,
    shift_two,
    mix_weight,
    head_weight,
    head_bias,
    species,
    counts,
):
    seq_count = lax.axis_size("seq")
    ch_count = lax.axis_size("ch")
    seq_index = lax.axis_index("seq")
    ch_index = lax.axis_index("ch")
    local_rows = inputs.shape[0]
    width = inputs.shape[1]
    conv_cols = conv_weight.shape[2]
    residual_rows = local_rows * ch_count
    every_bin_list = residual_rows * seq_count
    inv_bins = 1.0 / every_bin_list
    input_f = inputs.astype(jnp.float32)
    sum_one, square_one = lax.psum(
        (jnp.sum(input_f, 0), jnp.sum(input_f * input_f, 0)), ("seq", "ch")
    )
    mean_one = sum_one * inv_bins
    scale_one = lax.rsqrt(square_one * inv_bins - mean_one * mean_one + norm_eps)
    normed_one = (input_f - mean_one) * scale_one
    pre_one = normed_one * gain_one + shift_one
    act_one = jax.nn.gelu(pre_one).astype(jnp.bfloat16)
    residual_block = lax.all_gather(act_one, "ch", axis=0, tiled=True)
    padded_input = with_halo(residual_block, (("seq", 0),), DILATION_STEP)
    bin_positions = seq_index * residual_rows + jnp.arange(residual_rows, dtype=jnp.int32)
    local_window = window_lookup(bin_positions, every_bin_list)
    fwd_masks = [
        window_lookup(bin_positions + (kernel_tap_index - 1) * DILATION_STEP, every_bin_list)
        == local_window
        for kernel_tap_index in range(TAPS)
    ]
    back_masks = [
        (
            window_lookup(bin_positions - (kernel_tap_index - 1) * DILATION_STEP, every_bin_list)
            == local_window
        ).astype(jnp.float32)[:, None]
        for kernel_tap_index in range(TAPS)
    ]
    conv_out = jnp.zeros((residual_rows, conv_cols), jnp.float32)
    for kernel_tap_index in range(TAPS):
        product = jnp.dot(
            padded_input[
                kernel_tap_index * DILATION_STEP : kernel_tap_index * DILATION_STEP + residual_rows
            ],
            conv_weight[kernel_tap_index],
            preferred_element_type=jnp.float32,
        )
        conv_out = conv_out + jnp.where(fwd_masks[kernel_tap_index][:, None], product, 0.0)
    sum_two, square_two = lax.psum((jnp.sum(conv_out, 0), jnp.sum(conv_out * conv_out, 0)), "seq")
    mean_two = sum_two * inv_bins
    scale_two = lax.rsqrt(square_two * inv_bins - mean_two * mean_two + norm_eps)
    normed_two = (conv_out - mean_two) * scale_two
    pre_two = normed_two * gain_two + shift_two
    act_two = jax.nn.gelu(pre_two).astype(jnp.bfloat16)
    branch = lax.psum_scatter(
        jnp.dot(act_two, mix_weight, preferred_element_type=jnp.float32).astype(jnp.bfloat16),
        "ch",
        scatter_dimension=0,
        tiled=True,
    ).astype(jnp.float32)
    outputs = (input_f + branch).astype(jnp.bfloat16)
    row_start = seq_index * residual_rows + ch_index * local_rows
    window_index = window_lookup(row_start, every_bin_list)
    window_ids = jnp.arange(species.shape[0], dtype=jnp.int32)
    my_species = jnp.sum(jnp.where(window_ids == window_index, species, 0))
    is_human = my_species == 0
    targets = counts.astype(jnp.float32)
    zero_human = jnp.zeros((local_rows, HUMAN), jnp.bfloat16)
    zero_mouse = jnp.zeros((local_rows, MOUSE), jnp.bfloat16)
    start_logits = (
        jnp.zeros((local_rows, HUMAN), jnp.float32),
        jnp.zeros((local_rows, MOUSE), jnp.float32),
    )
    piece = lax.all_gather(head_weight, "ch", axis=0, tiled=True)

    def human_add(unused):
        return (
            jnp.dot(outputs, piece[:, :HUMAN], preferred_element_type=jnp.float32),
            start_logits[1],
        )

    def mouse_add(unused):
        return (
            start_logits[0],
            jnp.dot(outputs, piece[:, HUMAN:], preferred_element_type=jnp.float32),
        )

    logit_sums = lax.cond(is_human, human_add, mouse_add, 0)

    def human_grads(unused):
        return (poisson_grad(logit_sums[0] + head_bias[:HUMAN], targets), zero_mouse)

    def mouse_grads(unused):
        return (zero_human, poisson_grad(logit_sums[1] + head_bias[HUMAN:], targets[:, :MOUSE]))

    grad_human, grad_mouse = lax.cond(is_human, human_grads, mouse_grads, 0)

    def back_piece(piece):

        def human_back(unused):
            return lax.dot_general(
                grad_human, piece[:, :HUMAN], contract_cols, preferred_element_type=jnp.float32
            )

        def mouse_back(unused):
            return lax.dot_general(
                grad_mouse, piece[:, HUMAN:], contract_cols, preferred_element_type=jnp.float32
            )

        return lax.cond(is_human, human_back, mouse_back, 0)

    grad_out = back_piece(lax.all_gather(head_weight, "ch", axis=0, tiled=True))

    def human_term(unused):
        part = lax.dot_general(
            outputs, grad_human, contract_rows, preferred_element_type=jnp.float32
        )
        return jnp.concatenate(
            [
                part,
                jnp.zeros(
                    (lax.axis_size(("seq", "ch")) * (width // (seq_count * ch_count)), MOUSE),
                    jnp.float32,
                ),
            ],
            1,
        )

    def mouse_term(unused):
        part = lax.dot_general(
            outputs, grad_mouse, contract_rows, preferred_element_type=jnp.float32
        )
        return jnp.concatenate(
            [
                jnp.zeros(
                    (lax.axis_size(("seq", "ch")) * (width // (seq_count * ch_count)), HUMAN),
                    jnp.float32,
                ),
                part,
            ],
            1,
        )

    head_weight_grad = lax.psum_scatter(
        lax.cond(is_human, human_term, mouse_term, 0),
        ("seq", "ch"),
        scatter_dimension=0,
        tiled=True,
    )
    bias_part = jnp.concatenate(
        [jnp.sum(grad_human.astype(jnp.float32), 0), jnp.sum(grad_mouse.astype(jnp.float32), 0)]
    )
    grad_branch = grad_out.astype(jnp.bfloat16)
    mix_piece = lax.all_gather(grad_branch, "ch", axis=0, tiled=True)
    grad_rows = lax.dot_general(
        mix_piece, mix_weight, contract_cols, preferred_element_type=jnp.float32
    )
    grad_acts = grad_rows
    mix_part = lax.dot_general(
        act_two, mix_piece, contract_rows, preferred_element_type=jnp.float32
    )
    grad_pre_two = gelu_grad(pre_two, grad_acts)
    gain_part = jnp.sum(grad_pre_two * normed_two, 0)
    shift_part = jnp.sum(grad_pre_two, 0)
    gain_two_grad, shift_two_grad = lax.psum((gain_part, shift_part), "seq")
    convolution_gradient = (
        gain_two
        * scale_two
        * (grad_pre_two - shift_two_grad * inv_bins - normed_two * gain_two_grad * inv_bins)
    ).astype(jnp.bfloat16)
    padded_gradient = with_halo(convolution_gradient, (("seq", 0),), DILATION_STEP)
    conv_part = jnp.stack(
        [
            lax.dot_general(
                padded_input[
                    kernel_tap_index * DILATION_STEP : kernel_tap_index * DILATION_STEP
                    + residual_rows
                ],
                jnp.where(
                    fwd_masks[kernel_tap_index][:, None],
                    convolution_gradient,
                    jnp.zeros_like(convolution_gradient),
                ),
                contract_rows,
                preferred_element_type=jnp.float32,
            )
            for kernel_tap_index in range(TAPS)
        ]
    )
    total = jnp.zeros((lax.axis_size("ch") * local_rows, width), jnp.float32)
    for kernel_tap_index in range(TAPS):
        grad_rows = lax.dynamic_slice_in_dim(
            padded_gradient,
            (2 - kernel_tap_index) * DILATION_STEP,
            lax.axis_size("ch") * local_rows,
            0,
        )
        product = lax.dot_general(
            grad_rows,
            conv_weight[kernel_tap_index],
            contract_cols,
            preferred_element_type=jnp.float32,
        )
        total = total + product * back_masks[kernel_tap_index]
    grad_act_one = lax.psum_scatter(
        total.astype(jnp.bfloat16), "ch", scatter_dimension=0, tiled=True
    ).astype(jnp.float32)
    grad_pre_one = gelu_grad(pre_one, grad_act_one)
    gain_one_grad, shift_one_grad, head_bias_grad = lax.psum(
        (jnp.sum(grad_pre_one * normed_one, 0), jnp.sum(grad_pre_one, 0), bias_part), ("seq", "ch")
    )
    input_grad = grad_out + gain_one * scale_one * (
        grad_pre_one - shift_one_grad * inv_bins - normed_one * gain_one_grad * inv_bins
    )
    conv_weight_grad, mix_weight_grad = lax.psum((conv_part, mix_part), "seq")
    return (
        outputs,
        input_grad,
        gain_one_grad,
        shift_one_grad,
        conv_weight_grad,
        gain_two_grad,
        shift_two_grad,
        mix_weight_grad,
        head_weight_grad,
        head_bias_grad,
    )


def solution(mesh):
    in_specs = (
        P(("seq", "ch"), None),
        P(),
        P(),
        P(None, None, "ch"),
        P("ch"),
        P("ch"),
        P("ch", None),
        P("ch", None),
        P(),
        P(),
        P(("seq", "ch"), None),
    )
    out_specs = (
        P(("seq", "ch"), None),
        P(("seq", "ch"), None),
        P(),
        P(),
        P(None, None, "ch"),
        P("ch"),
        P("ch"),
        P("ch", None),
        P(("seq", "ch"), None),
        P(),
    )
    return jax.shard_map(
        on_device, mesh=mesh, in_specs=in_specs, out_specs=out_specs, check_vma=False
    )
```

profile of v0, /device:TPU:0, one launch (start us, length us, event | category | flops | bytes accessed | tf_op | source)
XLA Modules:
  0.0 632.3 jit_solution(14036912105792922197)
XLA Ops:
  7.3 1.2 convert_reduce_fusion.2
  8.4 42.1 %all-reduce.4 = (f32[768]{0:T(1024)S(1)}, f32[768]{0:T(1024)S(1)}) all-reduce(f32[768]{0:T(1024)S(1)} %get-tuple-element.95, f32[768]{0:T(1024)S(1)} %get-tuple-element.94), channel_id=1, replica_groups=mesh['seq'=8,'ch'=4] {'seq','ch'}, use_global_device_ids=true, to_apply=%region_3.0 | all-reduce | flops 1536 | bytes 12288 | tf_op jit(solution)/shard_map/psum | solution.py:71
  50.6 0.7 fusion.78
  51.2 2.1 fusion.33
  53.4 0.0 reduce-scatter.6.cloned.1.call-start
  53.5 19.5 %all-gather.4.cloned.1.call-done = bf16[1024,768]{1,0:T(8,128)(2,1)} async-done(((bf16[256,768]{1,0:T(8,128)(2,1)}), bf16[1024,768]{1,0:T(8,128)(2,1)}) %all-gather.4.cloned.1.call-update) | async-done | bytes 1572880 | tf_op jit(solution)/shard_map/all_gather | solution.py:79
  73.0 0.8 fusion.100
  73.8 1.5 collective-permute-start
  75.3 3.2 collective-permute-start.1
  78.6 2.0 fusion.58
  80.6 2.0 convolution_select_fusion
  82.7 0.7 fusion.97
  83.5 21.6 %all-reduce.6 = (f32[96]{0:T(128)S(1)}, f32[96]{0:T(128)S(1)}) all-reduce(f32[96]{0:T(128)S(1)} %get-tuple-element.93, f32[96]{0:T(128)S(1)} %get-tuple-element.92), channel_id=1, replica_groups=mesh['seq'=8,'ch'=4] {'seq'}, use_global_device_ids=true, to_apply=%region_7.8 | all-reduce | flops 192 | bytes 1536 | tf_op jit(solution)/shard_map/psum | solution.py:105
  105.1 1.9 convolution_convert_fusion
  107.1 0.7 all-gather.6.cloned.1.call-update
  107.9 0.6 fusion.82
  109.2 6.2 copy.26
  115.5 5.3 convert_element_type.74
  120.8 10.7 %reduce-scatter.6.cloned.1.call-done = bf16[256,768]{1,0:T(8,128)(2,1)} async-done(((bf16[1024,768]{1,0:T(8,128)(2,1)}), bf16[256,768]{1,0:T(8,128)(2,1)}) %reduce-scatter.6.cloned.1.call-update) | async-done | bytes 393232 | tf_op jit(solution)/shard_map/reduce_scatter | solution.py:111
  131.5 1.8 fusion.40
  133.3 71.9 %all-gather.6.cloned.1.call-done = bf16[768,6956]{1,0:T(8,128)(2,1)} async-done(((bf16[192,6956]{1,0:T(8,128)(2,1)}), bf16[768,6956]{1,0:T(8,128)(2,1)}) %all-gather.6.cloned.1.call-update) | async-done | bytes 10684432 | tf_op jit(solution)/shard_map/all_gather | solution.py:168
  205.3 4.7 conditional.4
  205.3 4.4 fusion
  209.6 0.4 broadcast_in_dim.41
  210.0 7.2 %conditional.5 = (bf16[256,5313]{1,0:T(8,128)(2,1)S(1)}, bf16[256,1643]{1,0:T(8,128)(2,1)}) conditional(s32[]{:T(128)} %convert_element_type.73, (f32[6956]{0:T(1024)S(1)}, f32[256,1643]{0,1:T(8,128)S(1)}, f32[256,5313]{1,0:T(8,128)}) %tuple.87, (f32[6956]{0:T(1024)S(1)}, f32[256,5313]{1,0:T(8,128)S(1)}, f32[256,5313]{1,0:T(8,128)}) %tuple.88), branch_computations={%region_12.13_spmd, %region_13.14_spmd} | conditional | flops 19041792 | bytes 17040690 | solution.py:152
  210.2 1.2 copy-done.3
  211.4 0.1 slice.43
  211.5 1.8 copy.27
  213.2 3.8 fusion.7
  217.0 0.2 broadcast_in_dim.46
  217.2 4.1 conditional.6
  217.2 4.1 fusion.12
  221.4 1.9 convert_element_type.75
  223.4 23.7 %all-gather.8.cloned.1.call-done = bf16[1024,768]{1,0:T(8,128)(2,1)} async-done(((bf16[256,768]{1,0:T(8,128)(2,1)}), bf16[1024,768]{1,0:T(8,128)(2,1)}) %all-gather.8.cloned.1.call-update) | async-done | bytes 1572880 | tf_op jit(solution)/shard_map/all_gather | solution.py:210
  247.1 3.0 fusion.96
  250.1 21.4 %all-reduce.5 = (f32[96]{0:T(128)S(1)}, f32[96]{0:T(128)S(1)}) all-reduce(f32[96]{0:T(128)S(1)} %get-tuple-element.91, f32[96]{0:T(128)S(1)} %get-tuple-element.90), channel_id=1, replica_groups=mesh['seq'=8,'ch'=4] {'seq'}, use_global_device_ids=true, to_apply=%region_19.20 | all-reduce | flops 192 | bytes 1536 | tf_op jit(solution)/shard_map/psum | solution.py:221
  271.5 1.4 multiply_convert_fusion
  272.9 0.1 fusion.101
  273.0 1.5 fusion.56
  274.5 2.1 collective-permute-start.3
  276.6 0.3 collective-permute-done.2
  276.9 0.7 fusion.48
  277.6 3.5 collective-permute-done.3
  281.1 2.2 add_convert_fusion
  283.3 0.3 all-reduce.10.cloned.1.call-start
  283.6 2.1 convolution_bitcast_fusion.2
  285.7 0.6 convolution_bitcast_fusion
  286.3 0.4 convolution_bitcast_fusion.1
  286.7 1.0 pad_maximum_fusion.6
  287.7 1.2 fusion.94
  289.0 13.7 %conditional.7 = (f32[768,6956]{0,1:T(8,128)}) conditional(s32[]{:T(128)} %convert_element_type.73, (bf16[256,768]{1,0:T(8,128)(2,1)}, bf16[256,1643]{1,0:T(8,128)(2,1)}) %tuple.41, (bf16[256,768]{1,0:T(8,128)(2,1)}, bf16[256,5313]{1,0:T(8,128)(2,1)S(1)}) %tuple.42), branch_computations={%region_27.28_spmd, %region_28.29_spmd} | conditional | flops 2089156608 | bytes 57125388 | solution.py:201
  289.0 2.2 fusion.102
  291.2 11.5 %concatenate.16 = f32[768,6956]{0,1:T(8,128)} pad(f32[768,1643]{0,1:T(8,128)S(1)} %fusion.102, f32[]{:T(128)} %constant.156.clone), padding=0_0x5313_0 | pad | bytes 26416132 | tf_op jit(solution)/shard_map/cond/branch_0_fun/concatenate | solution.py:189
  302.7 21.4 %copy.28 = f32[768,6956]{1,0:T(8,128)} copy(f32[768,6956]{0,1:T(8,128)} %get-tuple-element.145) | data formatting | bytes 42737664 | tf_op jit(solution)/shard_map/cond | solution.py:201
  324.2 1.3 convert_reduce_fusion.1
  325.5 0.5 convert_reduce_fusion
  325.9 0.1 pad_maximum_fusion.11
  326.0 1.8 fusion.95
  327.8 37.9 %all-reduce.3 = (f32[768]{0:T(1024)S(1)}, f32[768]{0:T(1024)S(1)}, f32[6956]{0:T(1024)}) all-reduce(f32[768]{0:T(1024)S(1)} %get-tuple-element.89, f32[768]{0:T(1024)S(1)} %get-tuple-element.88, f32[6956]{0:T(1024)S(1)} %pad_maximum_fusion.11), channel_id=1, replica_groups=mesh['seq'=8,'ch'=4] {'seq','ch'}, use_global_device_ids=true, to_apply=%region_24.25 | all-reduce | flops 8492 | bytes 67936 | tf_op jit(solution)/shard_map/psum | solution.py:265
  365.8 2.2 fusion.38
  368.0 24.2 %all-reduce.10.cloned.1.call-done = (f32[3,768,96]{1,2,0:T(8,128)}, f32[96,768]{1,0:T(8,128)}) async-done(((f32[3,768,96]{1,2,0:T(8,128)}, f32[96,768]{1,0:T(8,128)}), (f32[3,768,96]{1,2,0:T(8,128)}, f32[96,768]{1,0:T(8,128)})) %all-reduce.10.cloned.1.call-update) | async-done | bytes 1179664 | tf_op jit(solution)/shard_map/psum | solution.py:271
  392.2 229.4 %reduce-scatter.10.cloned.1.call-done = f32[24,6956]{1,0:T(8,128)} async-done(((f32[768,6956]{1,0:T(8,128)}), f32[24,6956]{1,0:T(8,128)}) %reduce-scatter.10.cloned.1.call-update) | async-done | bytes 667792
  621.6 2.1 copy.44
  623.8 1.7 copy.45
  (69 shorter events, 0.5 us)
Async XLA Ops:
  7.2 97.9 %copy-start = (bf16[96,768]{1,0:T(8,128)(2,1)S(1)}, bf16[96,768]{1,0:T(8,128)(2,1)}, u32[]{:S(2)}) copy-start(bf16[96,768]{1,0:T(8,128)(2,1)} %param.25) | copy-start | bytes 442372
  7.2 73.4 %copy-start.8 = (bf16[3,768,96]{1,2,0:T(8,128)(2,1)S(1)}, bf16[3,768,96]{1,2,0:T(8,128)(2,1)}, u32[]{:S(2)}) copy-start(bf16[3,768,96]{1,2,0:T(8,128)(2,1)} %param.22) | copy-start | bytes 1327108
  7.2 65.8 %all-gather.4.cloned.1.call-start = ((), (), s32[]{:S(2)}) async-start(), calls=%async_computation.3 | async-start | bytes 1966080 | tf_op jit(solution)/shard_map/all_gather | solution.py:79
  53.4 78.1 %reduce-scatter.6.cloned.1.call-start = ((), (), s32[]{:S(2)}) async-start(), calls=%async_computation.4 | async-start | bytes 1966080 | tf_op jit(solution)/shard_map/reduce_scatter | solution.py:111
  73.8 8.9 %collective-permute-start = (bf16[11,768]{1,0:T(8,128)(2,1)S(1)}, bf16[11,768]{1,0:T(8,128)(2,1)S(1)}, u32[]{:S(2)}, u32[]{:S(2)}) collective-permute-start(bf16[11,768]{1,0:T(8,128)(2,1)S(1)} %get-tuple-element.109), channel_id=1, source_target_pairs={{0,4},{4,8},{8,12},{12,16},{16,20},{20,24},{24,28},{28,0},{1,5},{5... | collective-permute-start | bytes 50696 | tf_op jit(solution)/shard_map/ppermute | solution.py:24
  75.3 7.4 %copy-start.4 = (bf16[1024,768]{1,0:T(8,128)(2,1)S(1)}, bf16[1024,768]{1,0:T(8,128)(2,1)}, u32[]{:S(2)}) copy-start(bf16[1024,768]{1,0:T(8,128)(2,1)} %all-gather.4.cloned.1.call-done) | copy-start | bytes 4718596
  75.3 5.3 collective-permute-start.1
  80.6 2.8 copy-start.21
  82.7 22.4 %copy-start.15 = (f32[96]{0:T(128)S(1)}, f32[96]{0:T(128)}, u32[]{:S(2)}) copy-start(f32[96]{0:T(128)} %param.23) | copy-start | bytes 1156
  82.7 22.4 %copy-start.17 = (f32[96]{0:T(128)S(1)}, f32[96]{0:T(128)}, u32[]{:S(2)}) copy-start(f32[96]{0:T(128)} %param.24) | copy-start | bytes 1156
  82.7 24.4 %copy-start.19 = (bf16[11,768]{1,0:T(8,128)(2,1)}, bf16[11,768]{1,0:T(8,128)(2,1)S(1)}, u32[]{:S(2)}) copy-start(bf16[11,768]{1,0:T(8,128)(2,1)S(1)} %collective-permute-done) | copy-start | bytes 50692
  83.5 24.4 %copy-start.6 = (f32[1024,96]{0,1:T(8,128)}, f32[1024,96]{0,1:T(8,128)S(1)}, u32[]{:S(2)}) copy-start(f32[1024,96]{0,1:T(8,128)S(1)} %get-tuple-element.119) | copy-start | bytes 1179652
  105.1 2.8 copy-start.23
  107.1 98.2 %all-gather.6.cloned.1.call-start = ((), (), s32[]{:S(2)}) async-start(), calls=%async_computation.5 | async-start | bytes 13516800 | tf_op jit(solution)/shard_map/all_gather | solution.py:168
  107.8 139.3 %all-gather.8.cloned.1.call-start = ((), (), s32[]{:S(2)}) async-start(), calls=%async_computation.6 | async-start | bytes 1966080 | tf_op jit(solution)/shard_map/all_gather | solution.py:210
  115.5 16.0 %copy-start.2 = (bf16[256,768]{1,0:T(8,128)(2,1)S(1)}, bf16[256,768]{1,0:T(8,128)(2,1)}, u32[]{:S(2)}) copy-start(bf16[256,768]{1,0:T(8,128)(2,1)} %param.19) | copy-start | bytes 1179652
  205.3 4.7 copy-start.10
  210.2 1.2 copy-start.3
  223.3 102.7 %reduce-scatter.8.cloned.1.call-start = ((), (), s32[]{:S(2)}) async-start(), calls=%async_computation.7 | async-start | bytes 1966080 | tf_op jit(solution)/shard_map/reduce_scatter | solution.py:261
  271.5 6.1 copy-start.16
  271.5 6.1 copy-start.24
  271.5 5.3 copy-start.9
  273.0 3.9 collective-permute-start.2
  274.5 6.6 %collective-permute-start.3 = (bf16[11,96]{0,1:T(8,128)(2,1)S(1)}, bf16[11,96]{0,1:T(8,128)(2,1)S(1)}, u32[]{:S(2)}, u32[]{:S(2)}) collective-permute-start(bf16[11,96]{0,1:T(8,128)(2,1)S(1)} %get-tuple-element.111), channel_id=1, source_target_pairs={{0,4},{4,8},{8,12},{12,16},{16,20},{20,24},{24,28},{28,0},{1,5},{5... | collective-permute-start | bytes 6344 | tf_op jit(solution)/shard_map/ppermute | solution.py:24
  281.1 2.5 copy-start.20
  283.3 2.4 copy-start.22
  283.3 108.9 %all-reduce.10.cloned.1.call-start = ((), (), s32[]{:S(2)}) async-start(), calls=%async_computation.9 | async-start | bytes 2359296 | tf_op jit(solution)/shard_map/psum | solution.py:271
  283.6 2.1 copy-start.5
  285.7 2.0 copy-start.7
  285.7 2.0 copy-start.18
  289.0 332.7 %reduce-scatter.10.cloned.1.call-start = ((), (), s32[]{:S(2)}) async-start(), calls=%async_computation.8 | async-start | bytes 22302720
  324.1 1.9 copy-start.11
  324.2 1.9 copy-start.12
  326.0 299.4 %copy-start.1 = (bf16[96,768]{1,0:T(8,128)(2,1)S(1)}, bf16[96,768]{1,0:T(8,128)(2,1)}, u32[]{:S(2)}) copy-start(bf16[96,768]{1,0:T(8,128)(2,1)} %param.25) | copy-start | bytes 442372
  365.8 259.7 %copy-start.13 = (f32[768]{0:T(1024)}, f32[768]{0:T(1024)S(1)}, u32[]{:S(2)}) copy-start(f32[768]{0:T(1024)S(1)} %get-tuple-element.134) | copy-start | bytes 9220
  365.8 259.7 %copy-start.14 = (f32[768]{0:T(1024)}, f32[768]{0:T(1024)S(1)}, u32[]{:S(2)}) copy-start(f32[768]{0:T(1024)S(1)} %get-tuple-element.135) | copy-start | bytes 9220
Sparse Core Ops, SparseCore 0:
  53.5 19.4 all-gather.3
  107.2 24.2 reduce-scatter.5
  133.1 72.0 all-gather.5
  223.4 23.6 all-gather.7
  283.4 24.4 reduce-scatter.7
  311.9 80.2 all-reduce.9
  400.4 221.2 reduce-scatter.9
where the time goes:
time: 634 us; the launch traced here: 632 us
  waiting for transfers between devices  384 us (61%)
  blocking collectives  123 us (19%)
  local copies, waits for them, and re-layouts  47.5 us (7%)
  matrix products  29.1 us (5%)
  other arithmetic  25.8 us (4%)
  between operations  15.2 us (2%)
  starting transfers between devices  7.34 us (1%)
    unnamed x8, waiting for transfers between devices  230 us
    all_gather x1, waiting for transfers between devices, on_device(): grad_out = back_piece(lax.all_gather(head_weight, 'ch', axis=0, tiled=True))  71.9 us
    psum x1, blocking collectives, on_device(): lax.psum((jnp.sum(input_f, 0), jnp.sum(input_f * input_f, 0)), ('seq', 'c...  42.1 us
    psum x1, blocking collectives, on_device(): lax.psum((jnp.sum(grad_pre_one * normed_one, 0), jnp.sum(grad_pre_one, 0)...  37.9 us
    psum x1, waiting for transfers between devices, on_device(): conv_weight_grad, mix_weight_grad = lax.psum((conv_part, mix_part), 'seq')  24.2 us
    all_gather x1, waiting for transfers between devices, on_device(): mix_piece = lax.all_gather(grad_branch, 'ch', axis=0, tiled=True)  23.7 us
    psum x1, blocking collectives, on_device(): lax.psum((jnp.sum(conv_out, 0), jnp.sum(conv_out * conv_out, 0)), 'seq')  21.6 us
    cond x1, local copies, waits for them, and re-layouts, on_device(): lax.cond(is_human, human_term, mouse_term, 0)  21.4 us
  transfers between devices with their start and end apart: 11, of which 8 were waited for; matrix products, arithmetic and copies ran while one was open for 11% of the time, Pallas kernels for 0%

commit v1 on v0

--- a/solution.py
+++ b/solution.py
@@ -1,3 +1,4 @@
+import functools
 import jax
 import jax.numpy as jnp
 from jax import lax
@@ -12,6 +13,25 @@
 norm_eps = 1e-05
 contract_rows = (((0,), (0,)), ((), ()))
 contract_cols = (((1,), (1,)), ((), ()))
+
+
+def arrange_arrays(body, net_axis):
+    a_now = jax.lax.axis_size(net_axis)
+    b_now = jax.lax.axis_index(net_axis)
+    far_arr, extra = (a_now, b_now)
+    built, tall = (body, 1)
+    while tall < far_arr:
+        all_values = jax.lax.ppermute(
+            built, net_axis, tuple(((u, u ^ tall) for u in range(far_arr)))
+        )
+        mixed_arr = jnp.concatenate([built, all_values], axis=0)
+        prior = jnp.concatenate([all_values, built], axis=0)
+        built = jnp.where(extra & tall == 0, mixed_arr, prior)
+        tall = 2 * tall
+    return built
+
+
+remake_stacks_all = functools.partial(arrange_arrays, net_axis="ch")
 
 
 def with_halo(cells, sides, width):
@@ -165,7 +185,7 @@
 
         return lax.cond(is_human, human_back, mouse_back, 0)
 
-    grad_out = back_piece(lax.all_gather(head_weight, "ch", axis=0, tiled=True))
+    grad_out = back_piece(remake_stacks_all(head_weight))
 
     def human_term(unused):
         part = lax.dot_general(

time: 634 us -> 754 us (1.19)
  waiting for transfers between devices: 384 us -> 466 us
  other arithmetic: 25.8 us -> 45.3 us
  local copies, waits for them, and re-layouts: 47.5 us -> 64.8 us
    ppermute x0 -> x2, waiting for transfers between devices: none -> 167 us  [arrange_arrays(): jax.lax.ppermute(built, net_axis, tuple(((u, u ^ tall) for u in range(far...]
    all_gather x1, waiting for transfers between devices: 71.9 us -> 0.01 us  [on_device(): piece = lax.all_gather(head_weight, 'ch', axis=0, tiled=True)]
    select_n x0 -> x2, other arithmetic: none -> 21.2 us  [arrange_arrays(): built = jnp.where(extra & tall == 0, mixed_arr, prior)]
    reduce_scatter x1, waiting for transfers between devices: 10.7 us -> 0.01 us  [on_device(): lax.psum_scatter(jnp.dot(act_two, mix_weight, preferred_element_type=jnp....]
    select_n x0 -> x1, local copies, waits for them, and re-layouts: none -> 8.2 us  [arrange_arrays(): built = jnp.where(extra & tall == 0, mixed_arr, prior)]
    ppermute x0 -> x1, local copies, waits for them, and re-layouts: none -> 8.07 us  [arrange_arrays(): jax.lax.ppermute(built, net_axis, tuple(((u, u ^ tall) for u in range(far...]
  transfers between devices with their start and end apart: 11 -> 13, of which waited for: 8 -> 8; matrix products, arithmetic and copies ran while one was open for 11% -> 14% of each run, Pallas kernels for 0% -> 0%
where the time goes in v1:
time: 754 us; the launch traced here: 753 us
  waiting for transfers between devices  466 us (62%)
  blocking collectives  123 us (16%)
  local copies, waits for them, and re-layouts  64.8 us (9%)
  other arithmetic  45.3 us (6%)
  matrix products  30.3 us (4%)
  between operations  15.2 us (2%)
  starting transfers between devices  7.6 us (1%)
    unnamed x8, waiting for transfers between devices  230 us
    ppermute x2, waiting for transfers between devices, arrange_arrays(): jax.lax.ppermute(built, net_axis, tuple(((u, u ^ tall) for u in range(far...  167 us
    psum x1, blocking collectives, on_device(): lax.psum((jnp.sum(input_f, 0), jnp.sum(input_f * input_f, 0)), ('seq', 'c...  42.1 us
    psum x1, blocking collectives, on_device(): lax.psum((jnp.sum(grad_pre_one * normed_one, 0), jnp.sum(grad_pre_one, 0)...  37.9 us
    psum x1, waiting for transfers between devices, on_device(): conv_weight_grad, mix_weight_grad = lax.psum((conv_part, mix_part), 'seq')  23.1 us
    all_gather x1, waiting for transfers between devices, on_device(): mix_piece = lax.all_gather(grad_branch, 'ch', axis=0, tiled=True)  22.7 us
    psum x1, blocking collectives, on_device(): lax.psum((jnp.sum(conv_out, 0), jnp.sum(conv_out * conv_out, 0)), 'seq')  21.6 us
    cond x1, local copies, waits for them, and re-layouts, on_device(): lax.cond(is_human, human_term, mouse_term, 0)  21.4 us
  transfers between devices with their start and end apart: 13, of which 8 were waited for; matrix products, arithmetic and copies ran while one was open for 14% of the time, Pallas kernels for 0%

profile of v1, /device:TPU:0, one launch (start us, length us, event | category | flops | bytes accessed | tf_op | source)
XLA Modules:
  0.0 752.6 jit_solution(9828747990214502687)
XLA Ops:
  7.3 1.2 convert_reduce_fusion.2
  8.4 42.1 %all-reduce.4 = (f32[768]{0:T(1024)S(1)}, f32[768]{0:T(1024)S(1)}) all-reduce(f32[768]{0:T(1024)S(1)} %get-tuple-element.104, f32[768]{0:T(1024)S(1)} %get-tuple-element.103), channel_id=1, replica_groups=mesh['seq'=8,'ch'=4] {'seq','ch'}, use_global_device_ids=true, to_apply=%region_3.0 | all-reduce | flops 1536 | bytes 12288 | tf_op jit(solution)/shard_map/psum | solution.py:91
  50.6 0.7 fusion.78
  51.2 2.1 fusion.33
  53.5 19.5 %all-gather.4.cloned.1.call-done = bf16[1024,768]{1,0:T(8,128)(2,1)} async-done(((bf16[256,768]{1,0:T(8,128)(2,1)}), bf16[1024,768]{1,0:T(8,128)(2,1)}) %all-gather.4.cloned.1.call-update) | async-done | bytes 1572880 | tf_op jit(solution)/shard_map/all_gather | solution.py:99
  73.0 0.9 fusion.100
  73.9 1.5 collective-permute-start
  75.4 3.2 collective-permute-start.1
  78.7 2.0 fusion.58
  80.8 2.0 convolution_select_fusion
  82.8 0.7 fusion.97
  83.6 21.6 %all-reduce.6 = (f32[96]{0:T(128)S(1)}, f32[96]{0:T(128)S(1)}) all-reduce(f32[96]{0:T(128)S(1)} %get-tuple-element.102, f32[96]{0:T(128)S(1)} %get-tuple-element.101), channel_id=1, replica_groups=mesh['seq'=8,'ch'=4] {'seq'}, use_global_device_ids=true, to_apply=%region_7.8 | all-reduce | flops 192 | bytes 1536 | tf_op jit(solution)/shard_map/psum | solution.py:125
  105.2 1.9 convolution_convert_fusion
  107.3 0.7 all-gather.6.cloned.1.call-update
  108.1 5.4 collective-permute-done.2
  113.5 7.2 maximum_select_fusion.1
  120.6 8.2 %copy.35 = bf16[384,6956]{0,1:T(8,128)(2,1)} copy(bf16[384,6956]{1,0:T(8,128)(2,1)} %maximum_select_fusion.1) | data formatting | bytes 10684416 | tf_op jit(solution)/shard_map/jit(_where)/select_n | solution.py:29
  128.8 0.2 collective-permute-start.3
  129.0 0.6 fusion.82
  130.3 6.1 copy.38
  136.4 5.3 convert_element_type.74
  141.7 1.1 fusion.40
  142.8 161.6 %collective-permute-done.3 = bf16[384,6956]{0,1:T(8,128)(2,1)} collective-permute-done((bf16[384,6956]{0,1:T(8,128)(2,1)}, bf16[384,6956]{0,1:T(8,128)(2,1)}, u32[]{:S(2)}, u32[]{:S(2)}) %collective-permute-start.3) | collective-permute-done | bytes 5342240 | tf_op jit(solution)/shard_map/ppermute | solution.py:24
  304.4 8.1 %copy.36 = bf16[384,6956]{1,0:T(8,128)(2,1)} copy(bf16[384,6956]{0,1:T(8,128)(2,1)} %collective-permute-done.3) | data formatting | bytes 10684416 | tf_op jit(solution)/shard_map/ppermute | solution.py:24
  312.5 14.1 %maximum_select_fusion = bf16[768,6956]{1,0:T(8,128)(2,1)} fusion(bf16[384,6956]{1,0:T(8,128)(2,1)} %copy.36, bf16[384,6956]{1,0:T(8,128)(2,1)} %maximum_select_fusion.1, pred[]{:T(512)S(6)} %eq.54), kind=kLoop, calls=%fused_computation.18 | loop fusion | flops 48079872 | bytes 21368832 | tf_op jit(solution)/shard_map/jit(_where)/select_n | solution.py:29
  326.6 4.8 conditional.4
  326.6 4.2 fusion
  330.8 0.4 broadcast_in_dim.41
  331.4 6.1 conditional.5
  331.4 1.2 copy-done.6
  332.6 1.8 copy.39
  334.4 2.9 fusion.7
  337.5 0.9 copy-done.4
  338.4 3.9 conditional.6
  338.4 3.9 fusion.12
  342.3 1.9 convert_element_type.75
  344.3 22.7 %all-gather.8.cloned.1.call-done = bf16[1024,768]{1,0:T(8,128)(2,1)} async-done(((bf16[256,768]{1,0:T(8,128)(2,1)}), bf16[1024,768]{1,0:T(8,128)(2,1)}) %all-gather.8.cloned.1.call-update) | async-done | bytes 1572880 | tf_op jit(solution)/shard_map/all_gather | solution.py:230
  367.0 3.0 fusion.96
  370.0 21.4 %all-reduce.5 = (f32[96]{0:T(128)S(1)}, f32[96]{0:T(128)S(1)}) all-reduce(f32[96]{0:T(128)S(1)} %get-tuple-element.100, f32[96]{0:T(128)S(1)} %get-tuple-element.99), channel_id=1, replica_groups=mesh['seq'=8,'ch'=4] {'seq'}, use_global_device_ids=true, to_apply=%region_19.20 | all-reduce | flops 192 | bytes 1536 | tf_op jit(solution)/shard_map/psum | solution.py:241
  391.4 1.4 multiply_convert_fusion
  392.9 1.5 fusion.56
  394.4 2.3 collective-permute-start.5
  396.7 0.3 collective-permute-done.4
  397.0 0.7 fusion.48
  397.7 3.5 collective-permute-done.5
  401.2 2.2 add_convert_fusion
  403.5 2.1 convolution_bitcast_fusion.2
  405.6 2.2 convolution_bitcast_fusion
  407.8 0.4 convolution_bitcast_fusion.1
  408.2 1.0 pad_maximum_fusion.6
  409.2 1.2 fusion.94
  410.5 13.8 %conditional.7 = (f32[768,6956]{0,1:T(8,128)}) conditional(s32[]{:T(128)} %convert_element_type.73, (bf16[256,768]{1,0:T(8,128)(2,1)}, bf16[256,1643]{1,0:T(8,128)(2,1)}) %tuple.92, (bf16[256,768]{1,0:T(8,128)(2,1)}, bf16[256,5313]{1,0:T(8,128)(2,1)S(1)}) %tuple.93), branch_computations={%region_27.28_spmd, %region_28.29_spmd} | conditional | flops 2089156608 | bytes 57125388 | solution.py:221
  410.5 2.1 fusion.102
  412.6 11.6 %concatenate.24 = f32[768,6956]{0,1:T(8,128)} pad(f32[768,1643]{0,1:T(8,128)S(1)} %fusion.102, f32[]{:T(128)} %constant.158.clone), padding=0_0x5313_0 | pad | bytes 26416132 | tf_op jit(solution)/shard_map/cond/branch_0_fun/concatenate | solution.py:209
  424.3 21.4 %copy.40 = f32[768,6956]{1,0:T(8,128)} copy(f32[768,6956]{0,1:T(8,128)} %get-tuple-element.154) | data formatting | bytes 42737664 | tf_op jit(solution)/shard_map/cond | solution.py:221
  445.7 1.3 convert_reduce_fusion.1
  447.0 0.5 convert_reduce_fusion
  447.6 1.8 fusion.95
  449.3 37.9 %all-reduce.3 = (f32[768]{0:T(1024)S(1)}, f32[768]{0:T(1024)S(1)}, f32[6956]{0:T(1024)}) all-reduce(f32[768]{0:T(1024)S(1)} %get-tuple-element.98, f32[768]{0:T(1024)S(1)} %get-tuple-element.97, f32[6956]{0:T(1024)S(1)} %pad_maximum_fusion.11), channel_id=1, replica_groups=mesh['seq'=8,'ch'=4] {'seq','ch'}, use_global_device_ids=true, to_apply=%region_24.25 | all-reduce | flops 8492 | bytes 67936 | tf_op jit(solution)/shard_map/psum | solution.py:285
  487.2 2.3 fusion.38
  489.4 23.1 %all-reduce.10.cloned.1.call-done = (f32[3,768,96]{1,2,0:T(8,128)}, f32[96,768]{1,0:T(8,128)}) async-done(((f32[3,768,96]{1,2,0:T(8,128)}, f32[96,768]{1,0:T(8,128)}), (f32[3,768,96]{1,2,0:T(8,128)}, f32[96,768]{1,0:T(8,128)})) %all-reduce.10.cloned.1.call-update) | async-done | bytes 1179664 | tf_op jit(solution)/shard_map/psum | solution.py:291
  512.5 229.4 %reduce-scatter.10.cloned.1.call-done = f32[24,6956]{1,0:T(8,128)} async-done(((f32[768,6956]{1,0:T(8,128)}), f32[24,6956]{1,0:T(8,128)}) %reduce-scatter.10.cloned.1.call-update) | async-done | bytes 667792
  741.9 2.1 copy.56
  744.1 1.7 copy.57
  (83 shorter events, 1.1 us)
Async XLA Ops:
  7.2 98.0 %copy-start = (bf16[96,768]{1,0:T(8,128)(2,1)S(1)}, bf16[96,768]{1,0:T(8,128)(2,1)}, u32[]{:S(2)}) copy-start(bf16[96,768]{1,0:T(8,128)(2,1)} %param.25) | copy-start | bytes 442372
  7.2 73.5 %copy-start.11 = (bf16[3,768,96]{1,2,0:T(8,128)(2,1)S(1)}, bf16[3,768,96]{1,2,0:T(8,128)(2,1)}, u32[]{:S(2)}) copy-start(bf16[3,768,96]{1,2,0:T(8,128)(2,1)} %param.22) | copy-start | bytes 1327108
  7.2 65.8 %all-gather.4.cloned.1.call-start = ((), (), s32[]{:S(2)}) async-start(), calls=%async_computation.3 | async-start | bytes 1966080 | tf_op jit(solution)/shard_map/all_gather | solution.py:99
  53.4 88.3 %reduce-scatter.6.cloned.1.call-start = ((), (), s32[]{:S(2)}) async-start(), calls=%async_computation.4 | async-start | bytes 1966080 | tf_op jit(solution)/shard_map/reduce_scatter | solution.py:131
  73.0 9.8 %copy-start.7 = (bf16[1024,768]{1,0:T(8,128)(2,1)S(1)}, bf16[1024,768]{1,0:T(8,128)(2,1)}, u32[]{:S(2)}) copy-start(bf16[1024,768]{1,0:T(8,128)(2,1)} %all-gather.4.cloned.1.call-done) | copy-start | bytes 4718596
  73.9 8.9 %collective-permute-start = (bf16[11,768]{1,0:T(8,128)(2,1)S(1)}, bf16[11,768]{1,0:T(8,128)(2,1)S(1)}, u32[]{:S(2)}, u32[]{:S(2)}) collective-permute-start(bf16[11,768]{1,0:T(8,128)(2,1)S(1)} %get-tuple-element.118), channel_id=1, source_target_pairs={{0,4},{4,8},{8,12},{12,16},{16,20},{20,24},{24,28},{28,0},{1,5},{5... | collective-permute-start | bytes 50696 | tf_op jit(solution)/shard_map/ppermute | solution.py:44
  75.4 5.3 collective-permute-start.1
  80.7 2.9 copy-start.24
  80.7 24.4 %copy-start.18 = (f32[96]{0:T(128)S(1)}, f32[96]{0:T(128)}, u32[]{:S(2)}) copy-start(f32[96]{0:T(128)} %param.23) | copy-start | bytes 1156
  80.8 24.5 %copy-start.20 = (f32[96]{0:T(128)S(1)}, f32[96]{0:T(128)}, u32[]{:S(2)}) copy-start(f32[96]{0:T(128)} %param.24) | copy-start | bytes 1156
  82.8 24.4 %copy-start.22 = (bf16[11,768]{1,0:T(8,128)(2,1)}, bf16[11,768]{1,0:T(8,128)(2,1)S(1)}, u32[]{:S(2)}) copy-start(bf16[11,768]{1,0:T(8,128)(2,1)S(1)} %collective-permute-done) | copy-start | bytes 50692
  83.6 24.4 %copy-start.9 = (f32[1024,96]{0,1:T(8,128)}, f32[1024,96]{0,1:T(8,128)S(1)}, u32[]{:S(2)}) copy-start(f32[1024,96]{0,1:T(8,128)S(1)} %get-tuple-element.128) | copy-start | bytes 1179652
  105.2 2.8 copy-start.2
  107.2 219.4 %all-gather.6.cloned.1.call-start = ((), (), s32[]{:S(2)}) async-start(), calls=%async_computation.5 | async-start | bytes 13516800 | tf_op jit(solution)/shard_map/all_gather | solution.py:150
  108.0 259.0 %all-gather.8.cloned.1.call-start = ((), (), s32[]{:S(2)}) async-start(), calls=%async_computation.6 | async-start | bytes 1966080 | tf_op jit(solution)/shard_map/all_gather | solution.py:230
  108.0 5.5 collective-permute-start.2
  120.6 8.4 %copy-start.26 = (s32[8]{0:T(128)S(1)}, s32[8]{0:T(128)}, u32[]{:S(2)}) copy-start(s32[8]{0:T(128)} %param.28) | copy-start | bytes 100
  128.8 175.6 %collective-permute-start.3 = (bf16[384,6956]{0,1:T(8,128)(2,1)}, bf16[384,6956]{0,1:T(8,128)(2,1)}, u32[]{:S(2)}, u32[]{:S(2)}) collective-permute-start(bf16[384,6956]{0,1:T(8,128)(2,1)} %copy.35), channel_id=1, source_target_pairs={{0,2},{1,3},{2,0},{3,1},{4,6},{5,7},{6,4},{7,5},{8,10},{9,11},{10,... | collective-permute-start | bytes 16026632 | tf_op jit(solution)/shard_map/ppermute | solution.py:24
  136.4 5.3 copy-start.3
  142.8 183.7 %copy-start.5 = (bf16[256,768]{1,0:T(8,128)(2,1)}, bf16[256,768]{1,0:T(8,128)(2,1)S(1)}, u32[]{:S(2)}) copy-start(bf16[256,768]{1,0:T(8,128)(2,1)S(1)} %fusion.40) | copy-start | bytes 1179652
  326.6 4.8 copy-start.13
  331.4 1.2 copy-start.6
  337.5 0.9 copy-start.4
  344.2 103.3 %reduce-scatter.8.cloned.1.call-start = ((), (), s32[]{:S(2)}) async-start(), calls=%async_computation.7 | async-start | bytes 1966080 | tf_op jit(solution)/shard_map/reduce_scatter | solution.py:281
  391.4 6.3 copy-start.19
  391.4 6.3 copy-start.27
  391.4 5.6 copy-start.12
  392.9 4.1 collective-permute-start.4
  394.4 6.8 collective-permute-start.5
  401.2 2.3 copy-start.23
  403.4 2.2 copy-start.25
  403.4 109.1 %all-reduce.10.cloned.1.call-start = ((), (), s32[]{:S(2)}) async-start(), calls=%async_computation.9 | async-start | bytes 2359296 | tf_op jit(solution)/shard_map/psum | solution.py:291
  403.5 4.3 copy-start.8
  405.6 3.6 copy-start.10
  405.6 3.6 copy-start.21
  410.4 331.5 %reduce-scatter.10.cloned.1.call-start = ((), (), s32[]{:S(2)}) async-start(), calls=%async_computation.8 | async-start | bytes 22302720
  445.7 1.9 copy-start.14
  445.7 1.9 copy-start.15
  447.5 298.3 %copy-start.1 = (bf16[96,768]{1,0:T(8,128)(2,1)S(1)}, bf16[96,768]{1,0:T(8,128)(2,1)}, u32[]{:S(2)}) copy-start(bf16[96,768]{1,0:T(8,128)(2,1)} %param.25) | copy-start | bytes 442372
  487.2 258.6 %copy-start.16 = (f32[768]{0:T(1024)}, f32[768]{0:T(1024)S(1)}, u32[]{:S(2)}) copy-start(f32[768]{0:T(1024)S(1)} %get-tuple-element.143) | copy-start | bytes 9220
  487.2 258.6 %copy-start.17 = (f32[768]{0:T(1024)}, f32[768]{0:T(1024)S(1)}, u32[]{:S(2)}) copy-start(f32[768]{0:T(1024)S(1)} %get-tuple-element.144) | copy-start | bytes 9220
Sparse Core Ops, SparseCore 0:
  53.5 19.4 all-gather.3
  107.3 24.2 reduce-scatter.5
  133.2 134.4 all-gather.5
  344.3 22.6 all-gather.7
  403.5 24.4 reduce-scatter.7
  432.0 80.5 all-reduce.9
  520.7 221.2 reduce-scatter.9
